TPU v7x, 128 devices: a whole 4x4x4 slice. The times are simulated.
128 devices in a mesh: tp: 4 (over x), fsdp: 32 (over z, y, core).
Axes of the slice: x: 4, y: 4, z: 4, core: 2. Of those that a mesh axis runs over, the one named last changes fastest.
Arguments:
- emb_table: float32 [16384, 2304], P('tp', 'fsdp')
- tok_ids: int32 [32, 1024], P('fsdp')
- lab_ids: int32 [32, 1024], P('fsdp')
- h_last: bfloat16 [32, 1024, 2304], P('fsdp')
- g_embed: bfloat16 [32, 1024, 2304], P('fsdp')
- norm_w: float32 [2304], P('fsdp')
Outputs:
- output 1: bfloat16 [32, 1024, 2304], P('fsdp')
- output 2: float32 [], replicated
- output 3: bfloat16 [32, 1024, 2304], P('fsdp')
- output 4: float32 [2304], P('fsdp')
- output 5: float32 [16384, 2304], P('tp', 'fsdp')
All inputs are finite; a program needn't handle non-finite values.
Results may differ from a plain program's by a relative error of at most 0.001.
Values are sent between devices in bfloat16 or wider.
A program may use at most 1 GiB of HBM per device.

v0:
```python
import math
import jax
import jax.numpy as jnp
from jax import lax
from jax.sharding import PartitionSpec as P

SOFT_CAP = 30.0
NORM_EPS = 1e-6


def solution(mesh):
    fsdp_size = mesh.shape["fsdp"]

    def device_step(emb_shard, tok_ids, lab_ids, h_last, g_embed, norm_w):
        vocab_rows = emb_shard.shape[0]
        batch_loc, seq_len, width = h_last.shape
        tok_count = batch_loc * seq_len
        total_tokens = tok_count * fsdp_size
        row_start = lax.axis_index("tp") * vocab_rows
        vocab_iota = jnp.arange(vocab_rows, dtype=jnp.int32)
        emb_scale = jnp.asarray(math.sqrt(width), jnp.bfloat16).astype(jnp.float32)
        shard_bf = emb_shard.astype(jnp.bfloat16)

        table_look = lax.all_gather(shard_bf, "fsdp", axis=1, tiled=True)
        tok_local = tok_ids.reshape(tok_count) - row_start
        in_block = (tok_local >= 0) & (tok_local < vocab_rows)
        row_vals = jnp.take(table_look, jnp.clip(tok_local, 0, vocab_rows - 1), axis=0)
        row_vals = lax.psum(jnp.where(in_block[:, None], row_vals, jnp.zeros_like(row_vals)), "tp")
        x_emb = (row_vals.astype(jnp.float32) * emb_scale).astype(jnp.bfloat16)

        norm_gain = 1.0 + lax.all_gather(norm_w, "fsdp", axis=0, tiled=True)
        h_wide = h_last.reshape(tok_count, width).astype(jnp.float32)
        inv_rms = lax.rsqrt(jnp.mean(h_wide * h_wide, axis=1, keepdims=True) + NORM_EPS)
        h_norm = h_wide * inv_rms
        x_norm = (h_norm * norm_gain).astype(jnp.bfloat16)

        table_head = lax.all_gather(shard_bf, "fsdp", axis=1, tiled=True)
        logits = jnp.einsum("td,vd->tv", x_norm, table_head, preferred_element_type=jnp.float32)
        tanh_z = jnp.tanh(logits / SOFT_CAP)
        capped = SOFT_CAP * tanh_z
        exp_shift = jnp.exp(capped - SOFT_CAP)
        lab_hit = (lab_ids.reshape(tok_count) - row_start)[:, None] == vocab_iota[None, :]
        tok_stats = jnp.stack([jnp.sum(exp_shift, axis=1), jnp.sum(jnp.where(lab_hit, capped, 0.0), axis=1)])
        tok_stats = lax.psum(tok_stats, "tp")
        sum_exp = tok_stats[0]
        log_norm = jnp.log(sum_exp) + SOFT_CAP
        loss_val = lax.psum(jnp.sum(log_norm - tok_stats[1]), "fsdp") / total_tokens

        soft_prob = exp_shift / sum_exp[:, None]
        d_logits = ((soft_prob - lab_hit.astype(jnp.float32)) * (1.0 - tanh_z * tanh_z) / total_tokens).astype(jnp.bfloat16)
        d_xnorm = lax.psum(jnp.dot(d_logits, table_head, preferred_element_type=jnp.float32), "tp")
        g_dir = d_xnorm * norm_gain
        d_hidden = (inv_rms * (g_dir - h_norm * jnp.mean(g_dir * h_norm, axis=1, keepdims=True))).astype(jnp.bfloat16)
        d_norm_w = lax.psum_scatter(jnp.sum(d_xnorm * h_norm, axis=0), "fsdp", scatter_dimension=0, tiled=True)

        head_part = jnp.einsum("tv,td->vd", d_logits, x_norm, preferred_element_type=jnp.float32)
        d_head = lax.psum_scatter(head_part, "fsdp", scatter_dimension=1, tiled=True)
        tok_hit = (tok_local[:, None] == vocab_iota[None, :]).astype(jnp.bfloat16)
        look_part = jnp.einsum("tv,td->vd", tok_hit, g_embed.reshape(tok_count, width), preferred_element_type=jnp.float32)
        d_look = lax.psum_scatter(look_part, "fsdp", scatter_dimension=1, tiled=True)
        d_table = d_head + emb_scale * d_look
        return (x_emb.reshape(batch_loc, seq_len, width), loss_val, d_hidden.reshape(batch_loc, seq_len, width), d_norm_w, d_table)

    spec_tok = P("fsdp", None)
    spec_act = P("fsdp", None, None)
    return jax.shard_map(device_step, mesh=mesh, in_specs=(P("tp", "fsdp"), spec_tok, spec_tok, spec_act, spec_act, P("fsdp")), out_specs=(spec_act, P(), spec_act, P("fsdp"), P("tp", "fsdp")), check_vma=False)
```

profile of v0, /device:TPU:0, one launch (start us, length us, event | category | flops | bytes accessed | tf_op | source)
XLA Modules:
  0.0 845.7 jit_solution(13855212165241230365)
XLA Ops:
  7.2 0.0 all-gather.2.cloned.1.call-start
  7.2 2.1 convert_element_type.28
  9.4 0.0 all-gather.2.cloned.1.call-update
  9.4 0.0 all-reduce.6.cloned.1.call-start
  9.4 1.3 fusion.22
  11.4 0.9 dynamic-update-slice
  12.3 130.8 %all-reduce = f32[2304]{0:T(1024)S(1)} all-reduce(f32[2304]{0:T(1024)S(1)} %dynamic-update-slice), channel_id=1, replica_groups=mesh['tp'=4,'fsdp'=32] {'fsdp'}, use_global_device_ids=true, to_apply=%add | all-reduce | flops 2304 | bytes 18432
  143.1 0.7 compare_select_fusion
  143.8 0.7 broadcast_subtract_fusion
  144.5 3.3 fusion.12
  147.9 0.0 all-gather.2.cloned.1.call-done
  147.9 23.7 %copy.13 = bf16[4096,2304]{1,0:T(8,128)(2,1)} copy(bf16[4096,2304]{0,1:T(8,128)(2,1)} %all-gather.2.cloned.1.call-done) | data formatting | bytes 37748736 | tf_op jit(solution)/shard_map/all_gather | solution.py:24
  171.6 18.6 %gather_fusion = bf16[1024,2304]{1,0:T(8,128)(2,1)} fusion(bf16[4096,2304]{1,0:T(8,128)(2,1)} %copy.13, s32[1024]{0:T(1024)S(1)} %broadcast_clamp_fusion), kind=kCustom, calls=%fused_computation | custom fusion | bytes 9441280 | tf_op jit(solution)/shard_map/jit(_take)/gather | solution.py:27
  190.2 4.4 select_select_fusion
  194.5 0.0 all-reduce.6.cloned.1.call-update
  194.6 0.0 all-reduce.8.cloned.1.call-start
  194.6 28.8 %fusion.1 = (f32[1024]{0:T(1024)S(1)}, f32[1024]{0:T(1024)S(1)}, f32[1024,4096]{1,0:T(8,128)}) fusion(s32[1024]{0:T(1024)S(1)} %bitcast.35, bf16[4096,2304]{0,1:T(8,128)(2,1)} %all-gather.2.cloned.1.call-done, bf16[1,1024,2304]{2,1,0:T(8,128)(2,1)} %param.9, f32[2304]{0:T(1024)S(1)} %broadcast_add_fusion, f32[1024]{0:T(1024)S(1)} %add_rsqrt_fusion), kind=kOutput, calls=%fused_computation.8 | convolution fusion | flops 19366150144 | bytes 40395776 | tf_op jit(solution)/shard_map/td,vd->tv/dot_general | solution.py:38
  223.5 11.1 %psum.29 = f32[2,1024]{1,0:T(2,128)S(1)} all-reduce(f32[2,1024]{1,0:T(2,128)S(1)} %pad_maximum_fusion), channel_id=1, replica_groups=mesh['tp'=4,'fsdp'=32] {'tp'}, use_global_device_ids=true, to_apply=%region_4.5 | all-reduce | flops 2048 | bytes 16384 | tf_op jit(solution)/shard_map/psum | solution.py:44
  234.6 11.2 %multiply_convert_fusion = bf16[1024,4096]{1,0:T(8,128)(2,1)S(1)} fusion(f32[1024,4096]{1,0:T(8,128)} %get-tuple-element.19, f32[1024]{0:T(1024)S(1)} %bitcast.33, s32[1024]{0:T(1024)S(1)} %bitcast.36), kind=kLoop, calls=%fused_computation.2 | loop fusion | flops 50331648 | bytes 25174016 | tf_op jit(solution)/shard_map/convert_element_type | solution.py:50
  245.7 0.0 copy-start
  245.7 3.3 copy-done
  249.1 24.6 %fusion.23 = f32[1024,2304]{1,0:T(8,128)} fusion(bf16[1024,4096]{1,0:T(8,128)(2,1)S(1)} %multiply_convert_fusion, bf16[4096,2304]{0,1:T(8,128)(2,1)} %all-gather.2.cloned.1.call-done), kind=kOutput, calls=%fused_computation.45 | convolution fusion | flops 19327352832 | bytes 36700160 | tf_op jit(solution)/shard_map/dot_general | solution.py:51
  273.6 0.0 all-reduce.8.cloned.1.call-update
  273.6 0.0 reduce-scatter.5.cloned.1.call-start
  273.7 27.2 %fusion = f32[4096,2304]{0,1:T(8,128)} fusion(s32[1024]{0:T(1024)S(1)} %bitcast.38, bf16[1,1024,2304]{2,1,0:T(8,128)(2,1)} %param.10), kind=kOutput, calls=%fused_computation.7 | convolution fusion | flops 19331547136 | bytes 42471424 | tf_op jit(solution)/shard_map/tv,td->vd/dot_general | solution.py:59
  300.9 0.0 reduce-scatter.5.cloned.1.call-update
  301.0 0.3 reduce-scatter.3.cloned.1.call-start
  301.2 27.9 %fusion.17 = f32[4096,2304]{0,1:T(8,128)} fusion(bf16[1024,4096]{1,0:T(8,128)(2,1)} %copy-done, bf16[1,1024,2304]{2,1,0:T(8,128)(2,1)} %param.9, f32[2304]{0:T(1024)S(1)} %broadcast_add_fusion, f32[1024]{0:T(1024)S(1)} %add_rsqrt_fusion), kind=kOutput, calls=%fused_computation.28 | convolution fusion | flops 19336790016 | bytes 50869248 | tf_op jit(solution)/shard_map/tv,td->vd/dot_general | solution.py:56
  329.1 0.0 reduce-scatter.3.cloned.1.call-update
  329.8 0.6 subtract_reduce_fusion
  330.4 0.0 all-reduce.6.cloned.1.call-done
  330.4 5.4 fusion.14
  335.8 135.5 %all-reduce.8.cloned.1.call-done = f32[1024,2304]{1,0:T(8,128)} async-done(((f32[1024,2304]{1,0:T(8,128)}), f32[1024,2304]{1,0:T(8,128)}) %all-reduce.8.cloned.1.call-update) | async-done | bytes 9437200 | tf_op jit(solution)/shard_map/psum | solution.py:51
  471.3 6.4 fusion.11
  477.7 129.5 %all-reduce.2 = (f32[]{:T(128)}, f32[2304]{0:T(1024)S(1)}) all-reduce(f32[]{:T(128)} %subtract_reduce_fusion, f32[2304]{0:T(1024)S(1)} %get-tuple-element.7), channel_id=1, replica_groups=mesh['tp'=4,'fsdp'=32] {'fsdp'}, use_global_device_ids=true, to_apply=%region_6.7 | all-reduce | flops 2305 | bytes 18440 | tf_op jit(solution)/shard_map/psum | solution.py:47
  607.9 0.6 dynamic-slice.2
  608.4 7.6 fusion.15
  616.0 37.6 %reduce-scatter.5.cloned.1.call-done = f32[4096,72]{0,1:T(8,128)} async-done(((f32[4096,2304]{0,1:T(8,128)}), f32[4096,72]{0,1:T(8,128)}) %reduce-scatter.5.cloned.1.call-update) | async-done | bytes 1179664 | tf_op jit(solution)/shard_map/reduce_scatter | solution.py:60
  653.7 181.6 %reduce-scatter.3.cloned.1.call-done = f32[4096,72]{0,1:T(8,128)} async-done(((f32[4096,2304]{0,1:T(8,128)}), f32[4096,72]{0,1:T(8,128)}) %reduce-scatter.3.cloned.1.call-update) | async-done | bytes 1179664 | tf_op jit(solution)/shard_map/reduce_scatter | solution.py:57
  835.2 2.8 multiply_add_fusion
  (8 shorter events, 0.1 us)
Async XLA Ops:
  7.2 140.7 %all-gather.2.cloned.1.call-start = ((), (), s32[]{:S(2)}) async-start(), calls=%async_computation.2 | async-start | bytes 19464192 | tf_op jit(solution)/shard_map/all_gather | solution.py:24
  9.4 321.0 %all-reduce.6.cloned.1.call-start = ((), (), s32[]{:S(2)}) async-start(), calls=%async_computation.3 | async-start | bytes 9437184 | tf_op jit(solution)/shard_map/psum | solution.py:28
  194.6 276.7 %all-reduce.8.cloned.1.call-start = ((), (), s32[]{:S(2)}) async-start(), calls=%async_computation.4 | async-start | bytes 18874368 | tf_op jit(solution)/shard_map/psum | solution.py:51
  245.7 3.3 copy-start
  273.6 380.0 %reduce-scatter.5.cloned.1.call-start = ((), (), s32[]{:S(2)}) async-start(), calls=%async_computation.6 | async-start | bytes 38928384 | tf_op jit(solution)/shard_map/reduce_scatter | solution.py:60
  301.0 534.3 %reduce-scatter.3.cloned.1.call-start = ((), (), s32[]{:S(2)}) async-start(), calls=%async_computation.5 | async-start | bytes 38928384 | tf_op jit(solution)/shard_map/reduce_scatter | solution.py:57
Sparse Core Ops, SparseCore 0:
  10.8 80.4 all-gather.1
  194.7 97.3 all-reduce.5
  294.5 176.7 all-reduce.7
  475.1 178.4 reduce-scatter.4
  657.5 177.7 reduce-scatter.2
where the time goes:
time: 847 us; the launch traced here: 846 us
  waiting for transfers between devices  355 us (42%)
  blocking collectives  271 us (32%)
  matrix products  109 us (13%)
  local copies, waits for them, and re-layouts  48.4 us (6%)
  other arithmetic  45.2 us (5%)
  between operations  17 us (2%)
    reduce_scatter x1, waiting for transfers between devices, device_step(): lax.psum_scatter(head_part, 'fsdp', scatter_dimension=1, tiled=True)  182 us
    psum x1, waiting for transfers between devices, device_step(): lax.psum(jnp.dot(d_logits, table_head, preferred_element_type=jnp.float32...  136 us
    unnamed x1, blocking collectives  131 us
    psum x1, blocking collectives, device_step(): loss_val = lax.psum(jnp.sum(log_norm - tok_stats[1]), 'fsdp') / total_tokens  129 us
    reduce_scatter x1, waiting for transfers between devices, device_step(): lax.psum_scatter(look_part, 'fsdp', scatter_dimension=1, tiled=True)  37.6 us
    dot_general x1, matrix products, device_step(): jnp.einsum('td,vd->tv', x_norm, table_head, preferred_element_type=jnp.fl...  28.8 us
    dot_general x1, matrix products, device_step(): jnp.einsum('tv,td->vd', d_logits, x_norm, preferred_element_type=jnp.floa...  27.9 us
    dot_general x1, matrix products, device_step(): jnp.einsum('tv,td->vd', tok_hit, g_embed.reshape(tok_count, width), prefe...  27.2 us
  transfers between devices with their start and end apart: 5, of which 3 were waited for; matrix products, arithmetic and copies ran while one was open for 17% of the time, Pallas kernels for 0%

commit v1 on v0

v1 whole, which is shorter than its diff:
```python
import math
import jax
import jax.numpy as jnp
from jax import lax
from jax.sharding import PartitionSpec as P

SOFT_CAP = 30.0
NORM_EPS = 1e-6


def solution(mesh):
    fsdp_size = mesh.shape["fsdp"]
    tp_size = mesh.shape["tp"]
    up = [(i, (i + 1) % tp_size) for i in range(tp_size)]
    down = [(i, (i - 1) % tp_size) for i in range(tp_size)]

    def ring_reduce_scatter(part):
        me = lax.axis_index("tp")
        rows = part.shape[0] // tp_size
        half = rows // 2

        def rel(k, lo, n):
            return lax.dynamic_slice_in_dim(part, ((me + k) % tp_size) * rows + lo, n, 0)

        far_up = lax.ppermute(rel(2, 0, half), "tp", up)
        far_down = lax.ppermute(rel(2, half, half), "tp", down)
        to_up = jnp.concatenate([rel(1, 0, half) + far_up, rel(1, half, half)])
        to_down = jnp.concatenate([rel(3, 0, half), rel(3, half, half) + far_down])
        return rel(0, 0, rows) + lax.ppermute(to_up, "tp", up) + lax.ppermute(to_down, "tp", down)

    def ring_all_gather(block):
        me = lax.axis_index("tp")
        rows, width = block.shape
        half = rows // 2
        from_below = lax.ppermute(block, "tp", up)
        from_above = lax.ppermute(block, "tp", down)
        far_lo = lax.ppermute(from_below[:half], "tp", up)
        far_hi = lax.ppermute(from_above[half:], "tp", down)
        out = jnp.zeros((tp_size * rows, width), block.dtype)
        for k, piece, lo in ((0, block, 0), (3, from_below, 0), (1, from_above, 0), (2, far_lo, 0), (2, far_hi, half)):
            out = lax.dynamic_update_slice_in_dim(out, piece, ((me + k) % tp_size) * rows + lo, 0)
        return out

    def device_step(emb_shard, tok_ids, lab_ids, h_last, g_embed, norm_w):
        vocab_rows, cols = emb_shard.shape
        batch_loc, seq_len, width = h_last.shape
        tok_count = batch_loc * seq_len
        total_tokens = tok_count * fsdp_size
        quarter = tok_count // tp_size
        tp_id = lax.axis_index("tp")
        fsdp_id = lax.axis_index("fsdp")
        row_start = tp_id * vocab_rows
        vocab_iota = jnp.arange(vocab_rows, dtype=jnp.int32)
        emb_scale = jnp.asarray(math.sqrt(width), jnp.bfloat16).astype(jnp.float32)
        shard_bf = emb_shard.astype(jnp.bfloat16)

        table = lax.all_gather(shard_bf, "fsdp", axis=1, tiled=True)
        own_w = jnp.where(tp_id == 0, norm_w, 0.0)
        full_w = lax.psum(lax.dynamic_update_slice(jnp.zeros((width,), jnp.float32), own_w, (fsdp_id * cols,)), ("tp", "fsdp"))
        norm_gain = 1.0 + full_w

        tok_local = tok_ids.reshape(tok_count) - row_start
        in_block = (tok_local >= 0) & (tok_local < vocab_rows)
        row_vals = jnp.take(table, jnp.clip(tok_local, 0, vocab_rows - 1), axis=0)
        row_vals = jnp.where(in_block[:, None], row_vals, jnp.zeros_like(row_vals))
        row_vals = ring_all_gather(ring_reduce_scatter(row_vals))
        x_emb = (row_vals.astype(jnp.float32) * emb_scale).astype(jnp.bfloat16)

        h_wide = h_last.reshape(tok_count, width).astype(jnp.float32)
        inv_rms = lax.rsqrt(jnp.mean(h_wide * h_wide, axis=1, keepdims=True) + NORM_EPS)
        h_norm = h_wide * inv_rms
        x_norm = (h_norm * norm_gain).astype(jnp.bfloat16)

        logits = jnp.einsum("td,vd->tv", x_norm, table, preferred_element_type=jnp.float32)
        tanh_z = jnp.tanh(logits / SOFT_CAP)
        capped = SOFT_CAP * tanh_z
        exp_shift = jnp.exp(capped - SOFT_CAP)
        lab_hit = (lab_ids.reshape(tok_count) - row_start)[:, None] == vocab_iota[None, :]
        tok_stats = jnp.stack([jnp.sum(exp_shift, axis=1), jnp.sum(jnp.where(lab_hit, capped, 0.0), axis=1)])
        tok_stats = lax.psum(tok_stats, "tp")
        sum_exp = tok_stats[0]
        loss_rows = jnp.log(sum_exp) + SOFT_CAP - tok_stats[1]

        soft_prob = exp_shift / sum_exp[:, None]
        d_logits = ((soft_prob - lab_hit.astype(jnp.float32)) * (1.0 - tanh_z * tanh_z) / total_tokens).astype(jnp.bfloat16)

        head_part = jnp.einsum("tv,td->vd", d_logits, x_norm, preferred_element_type=jnp.float32)
        tok_hit = (tok_local[:, None] == vocab_iota[None, :]).astype(jnp.bfloat16)
        look_part = jnp.einsum("tv,td->vd", tok_hit, g_embed.reshape(tok_count, width), preferred_element_type=jnp.float32)
        d_table = lax.psum_scatter(head_part + emb_scale * look_part, "fsdp", scatter_dimension=1, tiled=True)

        d_xnorm = ring_reduce_scatter(jnp.dot(d_logits, table, preferred_element_type=jnp.float32))
        h_own = lax.dynamic_slice_in_dim(h_last.reshape(tok_count, width), tp_id * quarter, quarter, 0).astype(jnp.float32)
        r_own = lax.rsqrt(jnp.mean(h_own * h_own, axis=1, keepdims=True) + NORM_EPS)
        hn_own = h_own * r_own
        g_dir = d_xnorm * norm_gain
        d_own = (r_own * (g_dir - hn_own * jnp.mean(g_dir * hn_own, axis=1, keepdims=True))).astype(jnp.bfloat16)
        d_hidden = ring_all_gather(d_own)

        loss_own = jnp.sum(lax.dynamic_slice_in_dim(loss_rows, tp_id * quarter, quarter, 0))
        tail = jnp.concatenate([jnp.sum(d_xnorm * hn_own, axis=0), jnp.full((128,), loss_own)])
        tail = lax.psum(tail, ("tp", "fsdp"))
        loss_val = tail[width] / total_tokens
        d_norm_w = lax.dynamic_slice(tail, (fsdp_id * cols,), (cols,))
        return (x_emb.reshape(batch_loc, seq_len, width), loss_val, d_hidden.reshape(batch_loc, seq_len, width), d_norm_w, d_table)

    spec_tok = P("fsdp", None)
    spec_act = P("fsdp", None, None)
    return jax.shard_map(device_step, mesh=mesh, in_specs=(P("tp", "fsdp"), spec_tok, spec_tok, spec_act, spec_act, P("fsdp")), out_specs=(spec_act, P(), spec_act, P("fsdp"), P("tp", "fsdp")), check_vma=False)
```

time: 847 us -> 569 us (0.67)
  waiting for transfers between devices: 355 us -> 146 us
  blocking collectives: 271 us -> 150 us
  starting transfers between devices: 0.43 us -> 23.8 us
  local copies, waits for them, and re-layouts: 48.4 us -> 64 us
    reduce_scatter x2 -> x1, waiting for transfers between devices: 219 us -> 0.01 us  [device_step(): lax.psum_scatter(head_part + emb_scale * look_part, 'fsdp', scatter_dimen...]
    ppermute x0 -> x16, waiting for transfers between devices: none -> 137 us  [the longest x2 31.3 us: ring_all_gather(): from_above = lax.ppermute(block, 'tp', down)]
    psum x2 -> x0, waiting for transfers between devices: 136 us -> none  [the longest x1 136 us: device_step(): lax.psum(jnp.dot(d_logits, table_head, preferred_element_type=jnp.float32...]
    unnamed x1 -> x0, blocking collectives: 131 us -> none
    ppermute x0 -> x16, starting transfers between devices: none -> 23.7 us  [the longest x2 6.43 us: ring_all_gather(): from_above = lax.ppermute(block, 'tp', down)]
    psum x1 -> x2, blocking collectives: 129 us -> 139 us  [the longest x1 69.8 us: device_step(): tail = lax.psum(tail, ('tp', 'fsdp'))]
    all_gather x1, waiting for transfers between devices: 0.02 us -> 8.88 us  [device_step(): table = lax.all_gather(shard_bf, 'fsdp', axis=1, tiled=True)]
  transfers between devices with their start and end apart: 5 -> 18, of which waited for: 3 -> 7; matrix products, arithmetic and copies ran while one was open for 17% -> 20% of each run, Pallas kernels for 0% -> 0%
where the time goes in v1:
time: 569 us; the launch traced here: 562 us
  blocking collectives  150 us (26%)
  waiting for transfers between devices  146 us (26%)
  matrix products  115 us (20%)
  local copies, waits for them, and re-layouts  64 us (11%)
  other arithmetic  46.4 us (8%)
  starting transfers between devices  23.8 us (4%)
  between operations  16.4 us (3%)
    psum x1, blocking collectives, device_step(): tail = lax.psum(tail, ('tp', 'fsdp'))  69.8 us
    psum x1, blocking collectives, device_step(): lax.psum(lax.dynamic_update_slice(jnp.zeros((width,), jnp.float32), own_w...  69.5 us
    dot_general x1, matrix products, device_step(): jnp.einsum('tv,td->vd', tok_hit, g_embed.reshape(tok_count, width), prefe...  33.8 us
    ppermute x2, waiting for transfers between devices, ring_all_gather(): from_above = lax.ppermute(block, 'tp', down)  31.3 us
    ppermute x2, waiting for transfers between devices, ring_all_gather(): from_below = lax.ppermute(block, 'tp', up)  30.2 us
    dot_general x1, matrix products, device_step(): jnp.einsum('tv,td->vd', d_logits, x_norm, preferred_element_type=jnp.floa...  28.8 us
    dot_general x1, matrix products, device_step(): jnp.einsum('td,vd->tv', x_norm, table, preferred_element_type=jnp.float32)  28.8 us
    ppermute x2, waiting for transfers between devices, ring_reduce_scatter(): far_up = lax.ppermute(rel(2, 0, half), 'tp', up)  24.1 us
  transfers between devices with their start and end apart: 18, of which 7 were waited for; matrix products, arithmetic and copies ran while one was open for 20% of the time, Pallas kernels for 0%

profile of v1, /device:TPU:0, one launch (start us, length us, event | category | flops | bytes accessed | tf_op | source)
XLA Modules:
  0.0 562.1 jit_solution(4767162274997366598)
XLA Ops:
  7.2 2.1 convert_element_type.34
  9.5 0.8 fusion.20
  10.3 69.5 %psum.21 = f32[2304]{0:T(1024)S(1)} all-reduce(f32[2304]{0:T(1024)S(1)} %fusion.20), channel_id=1, replica_groups=mesh['tp'=4,'fsdp'=32] {'tp','fsdp'}, use_global_device_ids=true, to_apply=%region_1.2 | all-reduce | flops 2304 | bytes 18432 | tf_op jit(solution)/shard_map/psum | solution.py:59
  79.8 3.3 fusion.1
  83.2 8.9 %all-gather.2.cloned.1.call-done = bf16[4096,2304]{0,1:T(8,128)(2,1)} async-done(((bf16[4096,72]{0,1:T(8,128)(2,1)}), bf16[4096,2304]{0,1:T(8,128)(2,1)}) %all-gather.2.cloned.1.call-update) | async-done | bytes 18874384 | tf_op jit(solution)/shard_map/all_gather | solution.py:57
  92.1 28.8 %fusion = (f32[1024]{0:T(1024)S(1)}, f32[1024]{0:T(1024)S(1)}, f32[1024,4096]{1,0:T(8,128)}) fusion(s32[1024]{0:T(1024)S(1)} %bitcast.48, bf16[4096,2304]{0,1:T(8,128)(2,1)} %all-gather.2.cloned.1.call-done, bf16[1,1024,2304]{2,1,0:T(8,128)(2,1)} %param.9, f32[2304]{0:T(1024)S(1)} %broadcast_add_fusion, f32[1024]{0:T(1024)S(1)} %add_rsqrt_fusion), kind=kOutput, calls=%fused_computation.8 | convolution fusion | flops 19366150144 | bytes 40395776 | tf_op jit(solution)/shard_map/td,vd->tv/dot_general | solution.py:74
  120.9 10.7 %psum.22 = f32[2,1024]{1,0:T(2,128)S(1)} all-reduce(f32[2,1024]{1,0:T(2,128)S(1)} %pad_maximum_fusion.4), channel_id=1, replica_groups=mesh['tp'=4,'fsdp'=32] {'tp'}, use_global_device_ids=true, to_apply=%region_4.5 | all-reduce | flops 2048 | bytes 16384 | tf_op jit(solution)/shard_map/psum | solution.py:80
  131.5 0.6 fusion.22
  132.1 11.2 %multiply_convert_fusion = bf16[1024,4096]{1,0:T(8,128)(2,1)S(1)} fusion(f32[1024,4096]{1,0:T(8,128)} %get-tuple-element.28, f32[1024]{0:T(1024)S(1)} %bitcast.46, s32[1024]{0:T(1024)S(1)} %bitcast.49), kind=kLoop, calls=%fused_computation.3 | loop fusion | flops 50331648 | bytes 25174016 | tf_op jit(solution)/shard_map/convert_element_type | solution.py:85
  143.3 28.8 %fusion.16 = f32[4096,2304]{0,1:T(8,128)} fusion(bf16[1024,4096]{1,0:T(8,128)(2,1)S(1)} %multiply_convert_fusion, bf16[1,1024,2304]{2,1,0:T(8,128)(2,1)} %param.9, f32[2304]{0:T(1024)S(1)} %broadcast_add_fusion, f32[1024]{0:T(1024)S(1)} %add_rsqrt_fusion), kind=kOutput, calls=%fused_computation.33 | convolution fusion | flops 19336790016 | bytes 50869248 | tf_op jit(solution)/shard_map/tv,td->vd/dot_general | solution.py:87
  172.1 33.8 %multiply_add_fusion = f32[4096,2304]{0,1:T(8,128)} fusion(f32[4096,2304]{0,1:T(8,128)} %fusion.16, s32[1024]{0:T(1024)S(1)} %bitcast.51, bf16[1,1024,2304]{2,1,0:T(8,128)(2,1)} %param.10), kind=kOutput, calls=%fused_computation.1 | convolution fusion | flops 19350421504 | bytes 80220160 | tf_op jit(solution)/shard_map/tv,td->vd/dot_general | solution.py:89
  206.0 22.9 %copy.13 = bf16[4096,2304]{1,0:T(8,128)(2,1)} copy(bf16[4096,2304]{0,1:T(8,128)(2,1)} %all-gather.2.cloned.1.call-done) | data formatting | bytes 37748736 | tf_op jit(solution)/shard_map/all_gather | solution.py:57
  228.8 18.6 %gather_fusion = bf16[1024,2304]{1,0:T(8,128)(2,1)} fusion(bf16[4096,2304]{1,0:T(8,128)(2,1)} %copy.13, s32[1024]{0:T(1024)S(1)} %broadcast_clamp_fusion), kind=kCustom, calls=%fused_computation | custom fusion | bytes 9441280 | tf_op jit(solution)/shard_map/jit(_take)/gather | solution.py:64
  247.4 2.9 select_select_fusion
  250.4 2.2 copy-done
  252.7 23.9 %fusion.23 = f32[1024,2304]{1,0:T(8,128)S(1)} fusion(bf16[1024,4096]{1,0:T(8,128)(2,1)} %copy-done.2, bf16[4096,2304]{0,1:T(8,128)(2,1)} %all-gather.2.cloned.1.call-done), kind=kOutput, calls=%fused_computation.77 | convolution fusion | flops 19327352832 | bytes 36700160 | tf_op jit(solution)/shard_map/dot_general | solution.py:92
  276.6 3.6 copy-done.1
  280.3 0.8 collective-permute-start.8
  281.1 1.8 dynamic-slice_add_fusion.3
  282.9 0.1 pad_maximum_fusion.2
  283.0 0.4 collective-permute-start.1
  283.4 2.9 collective-permute-start.2
  286.3 24.1 %collective-permute-done.8 = f32[128,2304]{1,0:T(8,128)S(1)} collective-permute-done((f32[128,2304]{1,0:T(8,128)S(1)}, f32[128,2304]{1,0:T(8,128)S(1)}, u32[]{:S(2)}, u32[]{:S(2)}) %collective-permute-start.8) | collective-permute-done | bytes 1179680 | tf_op jit(solution)/shard_map/ppermute | solution.py:25
  310.4 2.7 dynamic-slice_add_fusion.1
  313.1 2.1 collective-permute-start.10
  315.2 1.2 dynamic-slice_add_fusion.2
  316.4 0.1 pad_maximum_fusion.3
  316.5 0.1 collective-permute-start.3
  316.6 1.6 pad_maximum_fusion
  318.2 2.0 collective-permute-start.9
  320.2 21.9 %collective-permute-done.10 = f32[128,2304]{1,0:T(8,128)S(1)} collective-permute-done((f32[128,2304]{1,0:T(8,128)S(1)}, f32[128,2304]{1,0:T(8,128)S(1)}, u32[]{:S(2)}, u32[]{:S(2)}) %collective-permute-start.10) | collective-permute-done | bytes 1179680 | tf_op jit(solution)/shard_map/ppermute | solution.py:26
  342.1 1.4 dynamic-slice_add_fusion
  343.5 1.5 pad_maximum_fusion.1
  345.0 3.2 collective-permute-start.11
  348.2 19.1 %collective-permute-done.3 = bf16[256,2304]{1,0:T(8,128)(2,1)S(1)} collective-permute-done((bf16[256,2304]{1,0:T(8,128)(2,1)S(1)}, bf16[256,2304]{1,0:T(8,128)(2,1)S(1)}, u32[]{:S(2)}, u32[]{:S(2)}) %collective-permute-start.3) | collective-permute-done | bytes 1179680 | tf_op jit(solution)/shard_map/ppermute | solution.py:29
  367.3 2.5 broadcast.131
  369.8 3.2 constant_dynamic-update-slice_fusion.4
  373.0 3.2 collective-permute-start.5
  376.3 1.6 fusion.15
  377.9 0.7 dynamic-slice_reduce_fusion
  378.6 30.2 %collective-permute-done.4 = bf16[256,2304]{1,0:T(8,128)(2,1)S(1)} collective-permute-done((bf16[256,2304]{1,0:T(8,128)(2,1)}, bf16[256,2304]{1,0:T(8,128)(2,1)S(1)}, u32[]{:S(2)}, u32[]{:S(2)}) %collective-permute-start.4) | collective-permute-done | bytes 1179680 | tf_op jit(solution)/shard_map/ppermute | solution.py:35
  408.9 31.3 %collective-permute-done.5 = bf16[256,2304]{1,0:T(8,128)(2,1)S(1)} collective-permute-done((bf16[256,2304]{1,0:T(8,128)(2,1)}, bf16[256,2304]{1,0:T(8,128)(2,1)S(1)}, u32[]{:S(2)}, u32[]{:S(2)}) %collective-permute-start.5) | collective-permute-done | bytes 1179680 | tf_op jit(solution)/shard_map/ppermute | solution.py:36
  440.2 2.2 collective-permute-start.7
  442.5 1.1 constant_dynamic-update-slice_fusion.3
  443.5 1.1 constant_dynamic-update-slice_fusion.2
  444.6 0.9 constant_dynamic-update-slice_fusion.1
  445.5 4.1 fusion.11
  449.6 0.3 reshape.124
  449.9 0.6 bitcast_dynamic-update-slice_fusion.2
  450.6 2.2 copy-done.3
  452.8 3.2 collective-permute-start.13
  456.0 0.9 constant_dynamic-update-slice_fusion
  456.8 5.4 fusion.5
  462.2 0.6 concatenate.19
  462.8 69.8 %psum.23 = f32[2432]{0:T(1024)} all-reduce(f32[2432]{0:T(1024)S(1)} %concatenate.19), channel_id=1, replica_groups=mesh['tp'=4,'fsdp'=32] {'tp','fsdp'}, use_global_device_ids=true, to_apply=%region_8.9 | all-reduce | flops 2432 | bytes 19456 | tf_op jit(solution)/shard_map/psum | solution.py:102
  532.6 1.2 slice.34
  533.8 1.3 dynamic_slice.67
  535.8 1.5 collective-permute-start.14
  537.3 1.9 collective-permute-start.15
  539.2 1.1 bitcast_dynamic-update-slice_fusion.1
  540.3 1.1 bitcast_dynamic-update-slice_fusion
  541.4 10.8 %collective-permute-done.14 = bf16[128,2304]{1,0:T(8,128)(2,1)S(1)} collective-permute-done((bf16[128,2304]{1,0:T(8,128)(2,1)S(1)}, bf16[128,2304]{1,0:T(8,128)(2,1)S(1)}, u32[]{:S(2)}, u32[]{:S(2)}) %collective-permute-start.14) | collective-permute-done | bytes 589856 | tf_op jit(solution)/shard_map/ppermute | solution.py:37
  552.2 0.9 bitcast_dynamic-update-slice_fusion.4
  553.1 0.9 bitcast_dynamic-update-slice_fusion.3
  (56 shorter events, 0.7 us)
Async XLA Ops:
  7.2 76.0 %copy-start.8 = (s32[1,1024]{1,0:T(1,128)S(1)}, s32[1,1024]{1,0:T(1,128)}, u32[]{:S(2)}) copy-start(s32[1,1024]{1,0:T(1,128)} %param.8) | copy-start | bytes 12292
  7.2 76.0 %copy-start.7 = (s32[1,1024]{1,0:T(1,128)S(1)}, s32[1,1024]{1,0:T(1,128)}, u32[]{:S(2)}) copy-start(s32[1,1024]{1,0:T(1,128)} %param.7) | copy-start | bytes 12292
  7.2 84.9 %all-gather.2.cloned.1.call-start = ((), (), s32[]{:S(2)}) async-start(), calls=%async_computation.1 | async-start | bytes 19464192 | tf_op jit(solution)/shard_map/all_gather | solution.py:57
  9.4 544.5 %reduce-scatter.2.cloned.1.call-start = ((), (), s32[]{:S(2)}) async-start(), calls=%async_computation.2 | async-start | bytes 38928384 | tf_op jit(solution)/shard_map/reduce_scatter | solution.py:90
  132.1 11.2 %copy-start.4 = (f32[1,1024]{1,0:T(1,128)}, f32[1,1024]{1,0:T(1,128)S(1)}, u32[]{:S(2)}) copy-start(f32[1,1024]{1,0:T(1,128)S(1)} %get-tuple-element.25) | copy-start | bytes 12292
  143.3 28.8 %copy-start.2 = (bf16[1024,4096]{1,0:T(8,128)(2,1)}, bf16[1024,4096]{1,0:T(8,128)(2,1)S(1)}, u32[]{:S(2)}) copy-start(bf16[1024,4096]{1,0:T(8,128)(2,1)S(1)} %multiply_convert_fusion) | copy-start | bytes 25165828
  250.3 2.2 copy-start
  252.6 28.6 %collective-permute-start = (bf16[128,2304]{1,0:T(8,128)(2,1)S(1)}, bf16[128,2304]{1,0:T(8,128)(2,1)S(1)}, u32[]{:S(2)}, u32[]{:S(2)}) collective-permute-start(bf16[128,2304]{1,0:T(8,128)(2,1)S(1)} %constant_dynamic-slice_fusion.7), channel_id=1, source_target_pairs={{0,32},{32,64},{64,96},{96,0},{1,33},{33,65},{65,97},{97,1},{2,34}... | collective-permute-start | bytes 1769480 | tf_op jit(solution)/shard_map/ppermute | solution.py:25
  276.6 3.6 copy-start.1
  280.3 30.1 %collective-permute-start.8 = (f32[128,2304]{1,0:T(8,128)S(1)}, f32[128,2304]{1,0:T(8,128)S(1)}, u32[]{:S(2)}, u32[]{:S(2)}) collective-permute-start(f32[128,2304]{1,0:T(8,128)S(1)} %constant_dynamic-slice_fusion.3), channel_id=1, source_target_pairs={{0,32},{32,64},{64,96},{96,0},{1,33},{33,65},{65,97},{97,1},{2,34}... | collective-permute-start | bytes 3538952 | tf_op jit(solution)/shard_map/ppermute | solution.py:25
  283.0 65.2 %collective-permute-start.1 = (bf16[256,2304]{1,0:T(8,128)(2,1)S(1)}, bf16[256,2304]{1,0:T(8,128)(2,1)S(1)}, u32[]{:S(2)}, u32[]{:S(2)}) collective-permute-start(bf16[256,2304]{1,0:T(8,128)(2,1)S(1)} %pad_maximum_fusion.2), channel_id=1, source_target_pairs={{0,32},{32,64},{64,96},{96,0},{1,33},{33,65},{65,97},{97,1},{2,34}... | collective-permute-start | bytes 3538952 | tf_op jit(solution)/shard_map/ppermute | solution.py:29
  283.4 31.8 %collective-permute-start.2 = (bf16[128,2304]{1,0:T(8,128)(2,1)S(1)}, bf16[128,2304]{1,0:T(8,128)(2,1)S(1)}, u32[]{:S(2)}, u32[]{:S(2)}) collective-permute-start(bf16[128,2304]{1,0:T(8,128)(2,1)S(1)} %get-tuple-element.21), channel_id=1, source_target_pairs={{0,96},{32,0},{64,32},{96,64},{1,97},{33,1},{65,33},{97,65},{2,98}... | collective-permute-start | bytes 1769480 | tf_op jit(solution)/shard_map/ppermute | solution.py:26
  313.1 28.9 %collective-permute-start.10 = (f32[128,2304]{1,0:T(8,128)S(1)}, f32[128,2304]{1,0:T(8,128)S(1)}, u32[]{:S(2)}, u32[]{:S(2)}) collective-permute-start(f32[128,2304]{1,0:T(8,128)S(1)} %get-tuple-element.17), channel_id=1, source_target_pairs={{0,96},{32,0},{64,32},{96,64},{1,97},{33,1},{65,33},{97,65},{2,98}... | collective-permute-start | bytes 3538952 | tf_op jit(solution)/shard_map/ppermute | solution.py:26
  316.5 50.8 %collective-permute-start.3 = (bf16[256,2304]{1,0:T(8,128)(2,1)S(1)}, bf16[256,2304]{1,0:T(8,128)(2,1)S(1)}, u32[]{:S(2)}, u32[]{:S(2)}) collective-permute-start(bf16[256,2304]{1,0:T(8,128)(2,1)S(1)} %pad_maximum_fusion.3), channel_id=1, source_target_pairs={{0,96},{32,0},{64,32},{96,64},{1,97},{33,1},{65,33},{97,65},{2,98}... | collective-permute-start | bytes 3538952 | tf_op jit(solution)/shard_map/ppermute | solution.py:29
  318.2 127.3 %collective-permute-start.9 = (f32[256,2304]{1,0:T(8,128)}, f32[256,2304]{1,0:T(8,128)}, u32[]{:S(2)}, u32[]{:S(2)}) collective-permute-start(f32[256,2304]{1,0:T(8,128)} %pad_maximum_fusion), channel_id=1, source_target_pairs={{0,32},{32,64},{64,96},{96,0},{1,33},{33,65},{65,97},{97,1},{2,34}... | collective-permute-start | bytes 7077896 | tf_op jit(solution)/shard_map/ppermute | solution.py:29
  345.0 100.5 %collective-permute-start.11 = (f32[256,2304]{1,0:T(8,128)}, f32[256,2304]{1,0:T(8,128)}, u32[]{:S(2)}, u32[]{:S(2)}) collective-permute-start(f32[256,2304]{1,0:T(8,128)} %pad_maximum_fusion.1), channel_id=1, source_target_pairs={{0,96},{32,0},{64,32},{96,64},{1,97},{33,1},{65,33},{97,65},{2,98}... | collective-permute-start | bytes 7077896 | tf_op jit(solution)/shard_map/ppermute | solution.py:29
  369.8 8.0 %copy-start.5 = (f32[1,1024]{1,0:T(1,128)S(1)}, f32[1,1024]{1,0:T(1,128)}, u32[]{:S(2)}) copy-start(f32[1,1024]{1,0:T(1,128)} %copy-done.4) | copy-start | bytes 12292
  369.8 8.0 %copy-start.6 = (f32[1,1024]{1,0:T(1,128)S(1)}, f32[1,1024]{1,0:T(1,128)}, u32[]{:S(2)}) copy-start(f32[1,1024]{1,0:T(1,128)} %get-tuple-element.24) | copy-start | bytes 12292
  369.8 75.7 %slice-start = ((s8[4718592]{0:T(1024)(128)(4,1)}), s8[524288]{0:T(1024)(128)(4,1)S(1)}, s32[]{:S(2)}) async-start(s8[4718592]{0:T(1024)(128)(4,1)} %bitcast.44), calls=%async_computation.3 | async-start | bytes 1048576
  373.0 35.8 %collective-permute-start.4 = (bf16[256,2304]{1,0:T(8,128)(2,1)}, bf16[256,2304]{1,0:T(8,128)(2,1)S(1)}, u32[]{:S(2)}, u32[]{:S(2)}) collective-permute-start(bf16[256,2304]{1,0:T(8,128)(2,1)} %get-tuple-element.13), channel_id=1, source_target_pairs={{0,32},{32,64},{64,96},{96,0},{1,33},{33,65},{65,97},{97,1},{2,34}... | collective-permute-start | bytes 3538952 | tf_op jit(solution)/shard_map/ppermute | solution.py:35
  373.0 67.2 %collective-permute-start.5 = (bf16[256,2304]{1,0:T(8,128)(2,1)}, bf16[256,2304]{1,0:T(8,128)(2,1)S(1)}, u32[]{:S(2)}, u32[]{:S(2)}) collective-permute-start(bf16[256,2304]{1,0:T(8,128)(2,1)} %get-tuple-element.13), channel_id=1, source_target_pairs={{0,96},{32,0},{64,32},{96,64},{1,97},{33,1},{65,33},{97,65},{2,98}... | collective-permute-start | bytes 3538952 | tf_op jit(solution)/shard_map/ppermute | solution.py:36
  378.6 66.9 %slice-start.1 = ((s8[4718592]{0:T(1024)(128)(4,1)}), s8[4194304]{0:T(1024)(128)(4,1)S(1)}, s32[]{:S(2)}) async-start(s8[4718592]{0:T(1024)(128)(4,1)} %bitcast.44), calls=%async_computation.4 | async-start | bytes 8388608
  408.8 35.8 %collective-permute-start.6 = (bf16[128,2304]{1,0:T(8,128)(2,1)S(1)}, bf16[128,2304]{1,0:T(8,128)(2,1)S(1)}, u32[]{:S(2)}, u32[]{:S(2)}) collective-permute-start(bf16[128,2304]{1,0:T(8,128)(2,1)S(1)} %slice.30), channel_id=1, source_target_pairs={{0,32},{32,64},{64,96},{96,0},{1,33},{33,65},{65,97},{97,1},{2,34}... | collective-permute-start | bytes 1769480 | tf_op jit(solution)/shard_map/ppermute | solution.py:37
  440.2 15.7 %collective-permute-start.7 = (bf16[128,2304]{1,0:T(8,128)(2,1)S(1)}, bf16[128,2304]{1,0:T(8,128)(2,1)S(1)}, u32[]{:S(2)}, u32[]{:S(2)}) collective-permute-start(bf16[128,2304]{1,0:T(8,128)(2,1)S(1)} %slice.31), channel_id=1, source_target_pairs={{0,96},{32,0},{64,32},{96,64},{1,97},{33,1},{65,33},{97,65},{2,98}... | collective-permute-start | bytes 1769480 | tf_op jit(solution)/shard_map/ppermute | solution.py:38
  450.5 2.2 copy-start.3
  452.7 83.0 %collective-permute-start.12 = (bf16[256,2304]{1,0:T(8,128)(2,1)S(1)}, bf16[256,2304]{1,0:T(8,128)(2,1)S(1)}, u32[]{:S(2)}, u32[]{:S(2)}) collective-permute-start(bf16[256,2304]{1,0:T(8,128)(2,1)S(1)} %get-tuple-element.10), channel_id=1, source_target_pairs={{0,32},{32,64},{64,96},{96,0},{1,33},{33,65},{65,97},{97,1},{2,34}... | collective-permute-start | bytes 3538952 | tf_op jit(solution)/shard_map/ppermute | solution.py:35
  452.8 84.5 %collective-permute-start.13 = (bf16[256,2304]{1,0:T(8,128)(2,1)S(1)}, bf16[256,2304]{1,0:T(8,128)(2,1)S(1)}, u32[]{:S(2)}, u32[]{:S(2)}) collective-permute-start(bf16[256,2304]{1,0:T(8,128)(2,1)S(1)} %get-tuple-element.10), channel_id=1, source_target_pairs={{0,96},{32,0},{64,32},{96,64},{1,97},{33,1},{65,33},{97,65},{2,98}... | collective-permute-start | bytes 3538952 | tf_op jit(solution)/shard_map/ppermute | solution.py:36
  535.8 16.4 %collective-permute-start.14 = (bf16[128,2304]{1,0:T(8,128)(2,1)S(1)}, bf16[128,2304]{1,0:T(8,128)(2,1)S(1)}, u32[]{:S(2)}, u32[]{:S(2)}) collective-permute-start(bf16[128,2304]{1,0:T(8,128)(2,1)S(1)} %slice.35), channel_id=1, source_target_pairs={{0,32},{32,64},{64,96},{96,0},{1,33},{33,65},{65,97},{97,1},{2,34}... | collective-permute-start | bytes 1769480 | tf_op jit(solution)/shard_map/ppermute | solution.py:37
  537.3 15.8 %collective-permute-start.15 = (bf16[128,2304]{1,0:T(8,128)(2,1)S(1)}, bf16[128,2304]{1,0:T(8,128)(2,1)S(1)}, u32[]{:S(2)}, u32[]{:S(2)}) collective-permute-start(bf16[128,2304]{1,0:T(8,128)(2,1)S(1)} %slice.36), channel_id=1, source_target_pairs={{0,96},{32,0},{64,32},{96,64},{1,97},{33,1},{65,33},{97,65},{2,98}... | collective-permute-start | bytes 1769480 | tf_op jit(solution)/shard_map/ppermute | solution.py:38
Sparse Core Ops, SparseCore 0:
  10.8 81.2 all-gather.1
  206.0 175.1 reduce-scatter.1
